TPU v7x, 32 devices: a whole 2x2x4 slice. The times are simulated.
32 devices in a mesh: grp: 2 (over y), row: 4 (over z), head: 2 (over x), br: 2 (over core).
Axes of the slice: x: 2, y: 2, z: 4, core: 2. Of those that a mesh axis runs over, the one named last changes fastest.
Arguments:
- pair_acts: float32 [16, 8, 128], P(('grp', 'row', 'head')), parts along dimension 0, may hold values from -6 to 6
- alignment: float32 [64, 8, 256], P(('grp', 'br'), ('row', 'head')), parts along dimension 0, may hold values from -6 to 6
- align_mask: int32 [64, 8], P('grp', ('row', 'head')), parts along dimension 0, may hold values from 0 to 1
- residue_mask: int32 [16], P('grp'), parts along dimension 0, may hold values from 0 to 1, as said below
- align_gain: float32 [256], replicated, may hold values from 0.25 to 1.75
- outer_in: float32 [256, 64], replicated, may hold values from -0.375 to 0.375
- outer_out: float32 [1024, 128], replicated, may hold values from -1 to 1
- tri_gain: float32 [2, 128], replicated, may hold values from 0.25 to 1.75
- tri_in: float32 [2, 128, 4, 128], P(None, None, 'br'), may hold values from -5 to 5
- tri_bias: float32 [2, 128, 4], P(None, None, 'br'), may hold values from -0.5 to 0.5
- tri_out: float32 [2, 4, 32, 128], P(None, 'br'), may hold values from -0.5 to 0.5
- pair_cotangent: float32 [16, 8, 128], P(('grp', 'row', 'head')), parts along dimension 0, may hold values from -6 to 6
Outputs:
- pair_out: float32 [16, 8, 128], P(('grp', 'row', 'head')), parts along dimension 0
- pair_grad: float32 [16, 8, 128], P(('grp', 'row', 'head')), parts along dimension 0
There are 2 independent parts, one for each index of `grp`. A program takes and returns all parts, laid end to end along the dimension named above; an argument that names none is the same for every part. Nothing has to cross between parts.
Inputs may be any that keep to these rules, and one draw needn't show every extreme that they name: `residue_mask`: 1 at residue 0, and 0 at one or more residues; `align_mask`: 1 at every residue of sequence 0 of each part.
All inputs are finite; a program needn't handle non-finite values.
Results may differ from a plain program's by a relative error of at most 0.0003.
Values sent between devices are 32-bit elements; how exact they have to be, the bound alone decides.
No kernel may reach another device: no remote copies, remote signals or barrier semaphores. Data moves between devices by JAX's collectives and lax.ppermute only.
A program may use at most 64 MiB of HBM per device.

v0:
```python
import jax
import jax.numpy as jnp
from jax import lax
from jax.sharding import PartitionSpec as P

OPC = 32
PRECISE = lax.Precision.HIGHEST
EPSILON = 1e-05
MASK_SHIFT = 1000000000.0


def normalize(values, scales):
    average = jnp.mean(values, axis=-1, keepdims=True)
    centred = values - average
    spread = jnp.mean(centred * centred, axis=-1, keepdims=True)
    return centred * lax.rsqrt(spread + EPSILON) * scales


def core_total(values):
    return lax.psum(values, "br")


def reorient(values):
    turned = jnp.swapaxes(values, 0, 1)
    return lax.all_to_all(turned, ("row", "head"), split_axis=0, concat_axis=1, tiled=True)


def prepare(values, scales, weight_in, weight_bias):
    normed = normalize(values, scales)
    projected = jnp.einsum("ijc,chd->ijhd", normed, weight_in, precision=PRECISE)
    bias_local = jnp.einsum("jkc,ch->hjk", normed, weight_bias, precision=PRECISE)
    return (projected, bias_local)


def attend(projected, bias_full, key_shift, weight_out):
    head_size = projected.shape[-1] // 4
    queries = projected[..., :head_size]
    key_proj = projected[..., head_size : 2 * head_size]
    value_proj = projected[..., 2 * head_size : 3 * head_size]
    gating = projected[..., 3 * head_size :]
    logits = jnp.einsum("ijhd,ikhd->ihjk", queries, key_proj, precision=PRECISE) * head_size ** (
        -0.5
    )
    logits = logits + bias_full[None] + key_shift
    attention = jax.nn.softmax(logits, axis=-1)
    attended = jnp.einsum("ihjk,ikhd->ijhd", attention, value_proj, precision=PRECISE)
    gated_out = jax.nn.sigmoid(gating) * attended
    return jnp.einsum("ijhd,hdc->ijc", gated_out, weight_out, precision=PRECISE)


def tri_forward(rows_in, scales, weight_in, weight_bias, weight_out, key_shift, pair_mask):

    def local_prep(values):
        return prepare(values, scales, weight_in, weight_bias)

    (projected, bias_local), pull_prep = jax.vjp(local_prep, rows_in)
    bias_full = lax.all_gather(bias_local, ("row", "head"), axis=1, tiled=True)

    def local_attend(proj_in, bias_in):
        return attend(proj_in, bias_in, key_shift, weight_out)

    partial_out, pull_attend = jax.vjp(local_attend, projected, bias_full)
    total_out = core_total(partial_out)
    return (rows_in + total_out * pair_mask, (pull_prep, pull_attend))


def tri_backward(grad_out, saved, pair_mask):
    pull_prep, pull_attend = saved
    grad_proj, grad_bias = pull_attend(grad_out * pair_mask)
    grad_local = lax.psum_scatter(grad_bias, ("row", "head"), scatter_dimension=1, tiled=True)
    (grad_rows,) = pull_prep((grad_proj, grad_local))
    return grad_out + core_total(grad_rows)


def body(
    pair_acts,
    alignment,
    align_mask,
    residue_mask,
    align_gain,
    outer_in,
    outer_out,
    tri_gain,
    tri_in,
    tri_bias,
    tri_out,
    pair_cotangent,
):
    row_count = pair_acts.shape[0]
    live = residue_mask.astype(jnp.float32)
    key_shift = (live - 1.0) * MASK_SHIFT
    row_live = lax.dynamic_slice_in_dim(
        live, lax.axis_index(("row", "head")) * row_count, row_count, 0
    )
    pair_mask = row_live[:, None, None] * live[None, :, None]
    seq_count = alignment.shape[0]
    mask_all = align_mask.astype(jnp.float32)
    mask_own = lax.dynamic_slice_in_dim(mask_all, lax.axis_index("br") * seq_count, seq_count, 0)
    normed = normalize(alignment, align_gain)
    projected = jnp.einsum("snc,ck->snk", normed, outer_in, precision=PRECISE)
    left_part = projected[..., :OPC] * mask_own[..., None]
    right_part = jnp.swapaxes(projected[..., OPC:] * mask_own[..., None], 1, 2)
    right_all, mask_cols = (
        lax.all_gather(right_part, ("row", "head"), axis=2, tiled=True),
        lax.all_gather(mask_all, ("row", "head"), axis=1, tiled=True),
    )
    counts = jnp.einsum("si,sj->ij", mask_all, mask_cols, precision=PRECISE)
    table = outer_out.reshape(OPC, OPC, outer_out.shape[-1])
    mixed_left = jnp.einsum("sip,pqc->siqc", left_part, table, precision=PRECISE)
    partial_outer = jnp.einsum("siqc,sqj->ijc", mixed_left, right_all, precision=PRECISE)
    outer_sum = core_total(partial_outer)
    pair_one = pair_acts + outer_sum / counts[..., None]
    pair_two, saved_start = tri_forward(
        pair_one, tri_gain[0], tri_in[0], tri_bias[0], tri_out[0], key_shift, pair_mask
    )
    turned_two = reorient(pair_two)
    turned_three, saved_end = tri_forward(
        turned_two, tri_gain[1], tri_in[1], tri_bias[1], tri_out[1], key_shift, pair_mask
    )
    pair_out = reorient(turned_three)
    grad_turned = reorient(pair_cotangent)
    grad_turned = tri_backward(grad_turned, saved_end, pair_mask)
    grad_two = reorient(grad_turned)
    pair_grad = tri_backward(grad_two, saved_start, pair_mask)
    return (pair_out, pair_grad)


def solution(mesh):
    in_specs = (
        P(("grp", "row", "head"), None, None),
        P(("grp", "br"), ("row", "head"), None),
        P("grp", ("row", "head")),
        P("grp"),
        P(),
        P(),
        P(),
        P(),
        P(None, None, "br", None),
        P(None, None, "br"),
        P(None, "br", None, None),
        P(("grp", "row", "head"), None, None),
    )
    out_specs = (P(("grp", "row", "head"), None, None), P(("grp", "row", "head"), None, None))
    return jax.shard_map(body, mesh=mesh, in_specs=in_specs, out_specs=out_specs, check_vma=False)
```

profile of v0, /device:TPU:0, one launch (start us, length us, event | category | flops | bytes accessed | tf_op | source)
XLA Modules:
  0.0 188.4 jit_solution(10134027815885279675)
XLA Ops:
  0.7 1.0 reduce_sum.121
  1.7 0.3 multiply_reduce_fusion
  2.0 0.7 convert_bitcast_fusion
  2.6 0.8 multiply_multiply_fusion
  3.4 0.1 convolution_bitcast_fusion.12
  3.7 32.3 %all_gather.12 = f32[16,32,8]{1,0,2:T(8,128)S(1)} all-gather(f32[16,32,1]{1,0,2:T(8,128)S(1)} %fusion.30), channel_id=1, replica_groups=mesh['grp'=2,'row'=4,'head'=2,'br'=2] {'row','head'}, dimensions={2}, use_global_device_ids=true | all-gather | bytes 18432 | tf_op jit(solution)/shard_map/all_gather | solution.py:104
  36.2 0.7 fusion.8
  36.9 0.7 convolution_bitcast_fusion.17
  37.6 2.5 %psum.35 = f32[1,8,128]{2,1,0:T(8,128)S(1)} all-reduce(f32[1,8,128]{2,1,0:T(8,128)S(1)} %convolution_bitcast_fusion.17), channel_id=1, replica_groups=mesh['grp'=2,'row'=4,'head'=2,'br'=2] {'br'}, use_global_device_ids=true, to_apply=%region_2.0 | all-reduce | flops 1024 | bytes 8192 | tf_op jit(solution)/shard_map/psum | solution.py:20
  40.0 20.4 %all-gather.2 = f32[8,1,32]{2,1,0:T(1,128)S(1)} all-gather(f32[1,1,32]{2,1,0:T(1,128)S(1)} %get-tuple-element.16), channel_id=1, replica_groups=mesh['grp'=2,'row'=4,'head'=2,'br'=2] {'row','head'}, dimensions={0}, use_global_device_ids=true | all-gather | bytes 1152 | tf_op jit(solution)/shard_map/all_gather | solution.py:105
  60.5 0.7 copy-done.8
  61.3 0.6 copy-done.7
  62.0 0.2 fusion.120
  62.1 0.2 multiply_reduce_fusion.4
  62.4 0.6 copy-done.9
  63.0 0.6 dynamic_slice.7
  63.6 0.6 broadcast_multiply_fusion.2
  64.2 0.2 convolution_bitcast_fusion.11
  64.5 0.5 copy-done.5
  64.9 0.2 convolution_bitcast_fusion.19
  65.1 16.3 %all-gather.3 = f32[8,8,2]{1,2,0:T(2,128)S(1)} all-gather(f32[1,8,2]{1,2,0:T(2,128)S(1)} %convolution_bitcast_fusion.19), channel_id=2, replica_groups=mesh['grp'=2,'row'=4,'head'=2,'br'=2] {'row','head'}, dimensions={0}, use_global_device_ids=true | all-gather | bytes 576 | tf_op jit(solution)/shard_map/all_gather | solution.py:57
  81.7 0.2 fusion.122
  81.9 0.2 convolution_bitcast_fusion.10
  82.1 0.4 copy-done.2
  82.5 0.3 convolution_bitcast_fusion.16
  82.8 2.5 %psum.36 = f32[1,8,128]{2,1,0:T(8,128)S(1)} all-reduce(f32[1,8,128]{2,1,0:T(8,128)S(1)} %convolution_bitcast_fusion.16), channel_id=1, replica_groups=mesh['grp'=2,'row'=4,'head'=2,'br'=2] {'br'}, use_global_device_ids=true, to_apply=%region_7.0 | all-reduce | flops 1024 | bytes 8192 | tf_op jit(solution)/shard_map/psum | solution.py:20
  85.2 0.7 multiply_add_fusion
  85.9 3.3 %all-to-all-start = ((f32[8,1,128]{2,1,0:T(1,128)}), f32[8,1,128]{2,1,0:T(1,128)S(1)}, u32[]{:S(2)}, u32[]{:S(2)}) async-start(f32[8,1,128]{2,1,0:T(1,128)} %bitcast.32), calls=%async_computation | async-start | bytes 8192 | tf_op jit(solution)/shard_map/all_to_all | solution.py:25
  89.3 0.6 copy-done.10
  89.9 0.6 dynamic-slice
  90.5 5.1 %all-to-all-done = f32[8,1,128]{2,1,0:T(1,128)S(1)} async-done(((f32[8,1,128]{2,1,0:T(1,128)}), f32[8,1,128]{2,1,0:T(1,128)S(1)}, u32[]{:S(2)}, u32[]{:S(2)}) %all-to-all-start) | async-done | bytes 4128 | tf_op jit(solution)/shard_map/all_to_all | solution.py:25
  95.6 3.3 %all-to-all-start.2 = ((f32[8,1,128]{2,1,0:T(1,128)}), f32[8,1,128]{2,1,0:T(1,128)S(1)}, u32[]{:S(2)}, u32[]{:S(2)}) async-start(f32[8,1,128]{2,1,0:T(1,128)} %bitcast.54), calls=%async_computation.2 | async-start | bytes 8192 | tf_op jit(solution)/shard_map/all_to_all | solution.py:25
  99.1 0.2 fusion.67
  99.5 20.9 %all-gather.4 = f32[8,8,2]{1,2,0:T(2,128)S(1)} all-gather(f32[1,8,2]{1,2,0:T(2,128)S(1)} %convolution_bitcast_fusion.18), channel_id=3, replica_groups=mesh['grp'=2,'row'=4,'head'=2,'br'=2] {'row','head'}, dimensions={0}, use_global_device_ids=true | all-gather | bytes 576 | tf_op jit(solution)/shard_map/all_gather | solution.py:57
  120.7 0.2 convolution_bitcast_fusion.9
  120.8 0.2 fusion.123
  121.1 0.2 convolution_bitcast_fusion.8
  121.4 0.2 fusion.20
  121.7 0.3 multiply_reduce_fusion.2
  122.1 0.2 convolution_bitcast_fusion.4
  122.4 0.2 convolution_bitcast_fusion.6
  122.7 17.4 %all-reduce.8 = f32[2,8,8]{2,0,1:T(2,128)S(1)} all-reduce(f32[2,8,8]{2,0,1:T(2,128)S(1)} %copy.49), channel_id=4, replica_groups=mesh['grp'=2,'row'=4,'head'=2,'br'=2] {'row','head'}, use_global_device_ids=true, to_apply=%region_14.0.clone | all-reduce | flops 128 | bytes 1024
  140.0 0.8 fusion.92
  140.9 0.4 multiply_reduce_fusion.3
  141.3 0.2 fusion.119
  141.6 2.5 %psum.38 = f32[1,8,128]{2,1,0:T(8,128)S(1)} all-reduce(f32[1,8,128]{2,1,0:T(8,128)S(1)} %add_bitcast_fusion), channel_id=1, replica_groups=mesh['grp'=2,'row'=4,'head'=2,'br'=2] {'br'}, use_global_device_ids=true, to_apply=%region_17.0 | all-reduce | flops 1024 | bytes 8192 | tf_op jit(solution)/shard_map/psum | solution.py:20
  144.0 0.6 bitcast_add_fusion.1
  144.6 3.3 %all-to-all-start.3 = ((f32[8,1,128]{2,1,0:T(1,128)}), f32[8,1,128]{2,1,0:T(1,128)S(1)}, u32[]{:S(2)}, u32[]{:S(2)}) async-start(f32[8,1,128]{2,1,0:T(1,128)} %bitcast.75), calls=%async_computation.3 | async-start | bytes 8192 | tf_op jit(solution)/shard_map/all_to_all | solution.py:25
  147.9 0.3 convolution_bitcast_fusion.15
  148.2 6.1 %all-to-all-done.3 = f32[8,1,128]{2,1,0:T(1,128)S(1)} async-done(((f32[8,1,128]{2,1,0:T(1,128)}), f32[8,1,128]{2,1,0:T(1,128)S(1)}, u32[]{:S(2)}, u32[]{:S(2)}) %all-to-all-start.3) | async-done | bytes 4128 | tf_op jit(solution)/shard_map/all_to_all | solution.py:25
  154.4 0.2 fusion.21
  154.6 0.3 multiply_reduce_fusion.1
  155.0 0.2 convolution_bitcast_fusion
  155.3 0.2 convolution_bitcast_fusion.2
  155.6 17.9 %all-reduce.9 = f32[2,8,8]{2,0,1:T(2,128)S(1)} all-reduce(f32[2,8,8]{2,0,1:T(2,128)S(1)} %copy.52), channel_id=5, replica_groups=mesh['grp'=2,'row'=4,'head'=2,'br'=2] {'row','head'}, use_global_device_ids=true, to_apply=%region_19.0.clone | all-reduce | flops 128 | bytes 1024
  173.5 0.8 fusion.91
  174.4 0.4 fusion.65
  174.8 0.2 fusion.118
  175.1 2.5 %all-reduce.10 = (f32[1,8,128]{2,1,0:T(8,128)S(1)}, f32[1,8,128]{2,1,0:T(8,128)S(1)}) all-reduce(f32[1,8,128]{2,1,0:T(8,128)S(1)} %convolution_bitcast_fusion.15, f32[1,8,128]{2,1,0:T(8,128)S(1)} %broadcast_add_fusion), channel_id=1, replica_groups=mesh['grp'=2,'row'=4,'head'=2,'br'=2] {'br'}, use_global_device_ids=true, to_apply=%region_12.0 | all-reduce | flops 2048 | bytes 16384 | tf_op jit(solution)/shard_map/psum | solution.py:20
  177.5 0.7 bitcast_add_fusion.2
  178.2 3.3 %all-to-all-start.1 = ((f32[8,1,128]{2,1,0:T(1,128)}), f32[8,1,128]{2,1,0:T(1,128)S(1)}, u32[]{:S(2)}, u32[]{:S(2)}) async-start(f32[8,1,128]{2,1,0:T(1,128)} %bitcast.52), calls=%async_computation.1 | async-start | bytes 8192 | tf_op jit(solution)/shard_map/all_to_all | solution.py:25
  181.5 0.6 bitcast_add_fusion
  182.1 5.8 %all-to-all-done.1 = f32[8,1,128]{2,1,0:T(1,128)S(1)} async-done(((f32[8,1,128]{2,1,0:T(1,128)}), f32[8,1,128]{2,1,0:T(1,128)S(1)}, u32[]{:S(2)}, u32[]{:S(2)}) %all-to-all-start.1) | async-done | bytes 4128 | tf_op jit(solution)/shard_map/all_to_all | solution.py:25
  187.9 0.6 copy.81
  (61 shorter events, 2.2 us)
Async XLA Ops:
  0.6 35.6 %copy-start = (f32[1024,128]{1,0:T(8,128)S(1)}, f32[1024,128]{1,0:T(8,128)}, u32[]{:S(2)}) copy-start(f32[1024,128]{1,0:T(8,128)} %param.18) | copy-start | bytes 1572868
  0.6 1.0 copy-start.3
  0.7 2.8 %copy-start.4 = (f32[256,64]{0,1:T(8,128)S(1)}, f32[256,64]{0,1:T(8,128)}, u32[]{:S(2)}) copy-start(f32[256,64]{0,1:T(8,128)} %param.17) | copy-start | bytes 196612
  36.9 24.4 %copy-start.1 = (f32[2,128,2,128]{3,2,1,0:T(2,128)S(1)}, f32[2,128,2,128]{3,2,1,0:T(2,128)}, u32[]{:S(2)}) copy-start(f32[2,128,2,128]{3,2,1,0:T(2,128)} %param.20) | copy-start | bytes 786436
  60.5 0.7 copy-start.8
  61.2 0.7 copy-start.7
  61.2 0.7 copy-start.6
  62.3 0.7 copy-start.9
  64.2 0.7 copy-start.5
  81.7 0.8 copy-start.2
  85.9 9.7 %all-to-all-start = ((f32[8,1,128]{2,1,0:T(1,128)}), f32[8,1,128]{2,1,0:T(1,128)S(1)}, u32[]{:S(2)}, u32[]{:S(2)}) async-start(f32[8,1,128]{2,1,0:T(1,128)} %bitcast.32), calls=%async_computation | async-start | bytes 8192 | tf_op jit(solution)/shard_map/all_to_all | solution.py:25
  89.2 0.7 copy-start.10
  95.6 25.7 %all-to-all-start.2 = ((f32[8,1,128]{2,1,0:T(1,128)}), f32[8,1,128]{2,1,0:T(1,128)S(1)}, u32[]{:S(2)}, u32[]{:S(2)}) async-start(f32[8,1,128]{2,1,0:T(1,128)} %bitcast.54), calls=%async_computation.2 | async-start | bytes 8192 | tf_op jit(solution)/shard_map/all_to_all | solution.py:25
  144.6 9.7 %all-to-all-start.3 = ((f32[8,1,128]{2,1,0:T(1,128)}), f32[8,1,128]{2,1,0:T(1,128)S(1)}, u32[]{:S(2)}, u32[]{:S(2)}) async-start(f32[8,1,128]{2,1,0:T(1,128)} %bitcast.75), calls=%async_computation.3 | async-start | bytes 8192 | tf_op jit(solution)/shard_map/all_to_all | solution.py:25
  178.2 9.7 %all-to-all-start.1 = ((f32[8,1,128]{2,1,0:T(1,128)}), f32[8,1,128]{2,1,0:T(1,128)S(1)}, u32[]{:S(2)}, u32[]{:S(2)}) async-start(f32[8,1,128]{2,1,0:T(1,128)} %bitcast.52), calls=%async_computation.1 | async-start | bytes 8192 | tf_op jit(solution)/shard_map/all_to_all | solution.py:25
where the time goes:
time: 189 us; the launch traced here: 188 us
  blocking collectives  135 us (71%)
  waiting for transfers between devices  17 us (9%)
  starting transfers between devices  13.2 us (7%)
  matrix products  8.39 us (4%)
  other arithmetic  7.59 us (4%)
  local copies, waits for them, and re-layouts  6.07 us (3%)
    all_gather x2, blocking collectives, tri_forward(): bias_full = lax.all_gather(bias_local, ('row', 'head'), axis=1, tiled=True)  37.2 us
    unnamed x2, blocking collectives  35.3 us
    all_gather x1, blocking collectives, body(): lax.all_gather(right_part, ('row', 'head'), axis=2, tiled=True)  32.3 us
    all_gather x1, blocking collectives, body(): lax.all_gather(mask_all, ('row', 'head'), axis=1, tiled=True)  20.4 us
    all_to_all x4, waiting for transfers between devices, reorient(): lax.all_to_all(turned, ('row', 'head'), split_axis=0, concat_axis=1, tile...  17 us
    all_to_all x4, starting transfers between devices, reorient(): lax.all_to_all(turned, ('row', 'head'), split_axis=0, concat_axis=1, tile...  13.2 us
    psum x4, blocking collectives, core_total(): return lax.psum(values, 'br')  9.82 us
    unnamed x26, local copies, waits for them, and re-layouts  4.8 us
  transfers between devices with their start and end apart: 4, of which 3 were waited for; matrix products, arithmetic and copies ran while one was open for 2% of the time, Pallas kernels for 0%

commit v1 on v0

--- a/solution.py
+++ b/solution.py
@@ -54,7 +54,12 @@
         return prepare(values, scales, weight_in, weight_bias)
 
     (projected, bias_local), pull_prep = jax.vjp(local_prep, rows_in)
-    bias_full = lax.all_gather(bias_local, ("row", "head"), axis=1, tiled=True)
+    bias_full = jnp.concatenate(
+        lax.all_to_all(
+            jnp.stack([bias_local] * lax.axis_size(("row", "head"))), ("row", "head"), 0, 0
+        ),
+        axis=1,
+    )
 
     def local_attend(proj_in, bias_in):
         return attend(proj_in, bias_in, key_shift, weight_out)

time: 189 us -> 173 us (0.915)
  blocking collectives: 135 us -> 98.5 us
  waiting for transfers between devices: 17 us -> 29.6 us
  starting transfers between devices: 13.2 us -> 20.5 us
    all_gather x2 -> x0, blocking collectives: 37.2 us -> none  [tri_forward(): bias_full = lax.all_gather(bias_local, ('row', 'head'), axis=1, tiled=True)]
    all_to_all x0 -> x2, waiting for transfers between devices: none -> 9.38 us  [tri_forward(): lax.all_to_all(jnp.stack([bias_local] * lax.axis_size(('row', 'head'))),...]
    all_to_all x0 -> x2, starting transfers between devices: none -> 6.66 us  [tri_forward(): lax.all_to_all(jnp.stack([bias_local] * lax.axis_size(('row', 'head'))),...]
    all_to_all x4, waiting for transfers between devices: 17 us -> 20.2 us  [reorient(): lax.all_to_all(turned, ('row', 'head'), split_axis=0, concat_axis=1, tile...]
    unnamed x26 -> x24, local copies, waits for them, and re-layouts: 4.8 us -> 4.1 us
  transfers between devices with their start and end apart: 4 -> 6, of which waited for: 3 -> 6; matrix products, arithmetic and copies ran while one was open for 2% -> 3% of each run, Pallas kernels for 0% -> 0%
where the time goes in v1:
time: 173 us; the launch traced here: 172 us
  blocking collectives  98.5 us (57%)
  waiting for transfers between devices  29.6 us (17%)
  starting transfers between devices  20.5 us (12%)
  matrix products  8.35 us (5%)
  other arithmetic  7.58 us (4%)
  local copies, waits for them, and re-layouts  6.44 us (4%)
    unnamed x2, blocking collectives  35.8 us
    all_gather x1, blocking collectives, body(): lax.all_gather(right_part, ('row', 'head'), axis=2, tiled=True)  32.3 us
    all_gather x1, blocking collectives, body(): lax.all_gather(mask_all, ('row', 'head'), axis=1, tiled=True)  20.4 us
    all_to_all x4, waiting for transfers between devices, reorient(): lax.all_to_all(turned, ('row', 'head'), split_axis=0, concat_axis=1, tile...  20.2 us
    all_to_all x4, starting transfers between devices, reorient(): lax.all_to_all(turned, ('row', 'head'), split_axis=0, concat_axis=1, tile...  13.8 us
    psum x4, blocking collectives, core_total(): return lax.psum(values, 'br')  9.82 us
    all_to_all x2, waiting for transfers between devices, tri_forward(): lax.all_to_all(jnp.stack([bias_local] * lax.axis_size(('row', 'head'))),...  9.38 us
    all_to_all x2, starting transfers between devices, tri_forward(): lax.all_to_all(jnp.stack([bias_local] * lax.axis_size(('row', 'head'))),...  6.66 us
  transfers between devices with their start and end apart: 6, of which 6 were waited for; matrix products, arithmetic and copies ran while one was open for 3% of the time, Pallas kernels for 0%

profile of v1, /device:TPU:0, one launch (start us, length us, event | category | flops | bytes accessed | tf_op | source)
XLA Modules:
  0.0 171.9 jit_solution(11429963420560062672)
XLA Ops:
  0.7 1.0 reduce_sum.121
  1.7 0.3 multiply_reduce_fusion
  2.0 0.7 convert_bitcast_fusion
  2.6 0.8 multiply_multiply_fusion
  3.7 32.3 %all_gather.6 = f32[16,32,8]{1,0,2:T(8,128)S(1)} all-gather(f32[16,32,1]{1,0,2:T(8,128)S(1)} %fusion.30), channel_id=1, replica_groups=mesh['grp'=2,'row'=4,'head'=2,'br'=2] {'row','head'}, dimensions={2}, use_global_device_ids=true | all-gather | bytes 18432 | tf_op jit(solution)/shard_map/all_gather | solution.py:109
  36.2 0.7 fusion.8
  36.9 0.7 convolution_bitcast_fusion.17
  37.6 2.5 %psum.35 = f32[1,8,128]{2,1,0:T(8,128)S(1)} all-reduce(f32[1,8,128]{2,1,0:T(8,128)S(1)} %convolution_bitcast_fusion.17), channel_id=1, replica_groups=mesh['grp'=2,'row'=4,'head'=2,'br'=2] {'br'}, use_global_device_ids=true, to_apply=%region_2.0 | all-reduce | flops 1024 | bytes 8192 | tf_op jit(solution)/shard_map/psum | solution.py:20
  40.0 20.4 %all-gather = f32[8,1,32]{2,1,0:T(1,128)S(1)} all-gather(f32[1,1,32]{2,1,0:T(1,128)S(1)} %get-tuple-element.16), channel_id=1, replica_groups=mesh['grp'=2,'row'=4,'head'=2,'br'=2] {'row','head'}, dimensions={0}, use_global_device_ids=true | all-gather | bytes 1152 | tf_op jit(solution)/shard_map/all_gather | solution.py:110
  60.6 0.6 copy-done.7
  61.6 0.7 copy-done.5
  62.2 0.2 convolution_bitcast_fusion.19
  62.4 0.6 stack.4
  63.0 3.3 %all-to-all-start = ((f32[8,2,1,8]{3,1,2,0:T(2,128)}), f32[8,2,1,8]{3,1,2,0:T(2,128)S(1)}, u32[]{:S(2)}, u32[]{:S(2)}) async-start(f32[8,2,1,8]{3,1,2,0:T(2,128)} %stack.4), calls=%async_computation | async-start | bytes 16384 | tf_op jit(solution)/shard_map/all_to_all | solution.py:58
  66.4 0.6 copy-done.9
  67.1 0.6 dynamic_slice.7
  67.6 0.6 broadcast_multiply_fusion.2
  68.3 0.2 convolution_bitcast_fusion.11
  68.5 0.7 copy-done.10
  69.2 0.6 dynamic-slice
  69.8 3.1 %all-to-all-done = f32[8,2,1,8]{3,1,2,0:T(2,128)S(1)} async-done(((f32[8,2,1,8]{3,1,2,0:T(2,128)}), f32[8,2,1,8]{3,1,2,0:T(2,128)S(1)}, u32[]{:S(2)}, u32[]{:S(2)}) %all-to-all-start) | async-done | bytes 544 | tf_op jit(solution)/shard_map/all_to_all | solution.py:58
  72.8 3.3 %all-to-all-start.4 = ((f32[8,1,128]{2,1,0:T(1,128)}), f32[8,1,128]{2,1,0:T(1,128)S(1)}, u32[]{:S(2)}, u32[]{:S(2)}) async-start(f32[8,1,128]{2,1,0:T(1,128)} %bitcast.58), calls=%async_computation.4 | async-start | bytes 8192 | tf_op jit(solution)/shard_map/all_to_all | solution.py:25
  76.2 0.2 fusion.122
  76.5 0.2 convolution_bitcast_fusion.10
  76.7 0.4 copy-done.2
  77.1 0.3 convolution_bitcast_fusion.16
  77.4 2.5 %psum.36 = f32[1,8,128]{2,1,0:T(8,128)S(1)} all-reduce(f32[1,8,128]{2,1,0:T(8,128)S(1)} %convolution_bitcast_fusion.16), channel_id=1, replica_groups=mesh['grp'=2,'row'=4,'head'=2,'br'=2] {'br'}, use_global_device_ids=true, to_apply=%region_7.0 | all-reduce | flops 1024 | bytes 8192 | tf_op jit(solution)/shard_map/psum | solution.py:20
  79.8 0.7 multiply_add_fusion
  80.5 2.0 %all-to-all-done.4 = f32[8,1,128]{2,1,0:T(1,128)S(1)} async-done(((f32[8,1,128]{2,1,0:T(1,128)}), f32[8,1,128]{2,1,0:T(1,128)S(1)}, u32[]{:S(2)}, u32[]{:S(2)}) %all-to-all-start.4) | async-done | bytes 4128 | tf_op jit(solution)/shard_map/all_to_all | solution.py:25
  82.5 3.9 %all-to-all-start.1 = ((f32[8,1,128]{2,1,0:T(1,128)}), f32[8,1,128]{2,1,0:T(1,128)S(1)}, u32[]{:S(2)}, u32[]{:S(2)}) async-start(f32[8,1,128]{2,1,0:T(1,128)} %bitcast.34), calls=%async_computation.1 | async-start | bytes 8192 | tf_op jit(solution)/shard_map/all_to_all | solution.py:25
  86.5 6.3 %all-to-all-done.1 = f32[8,1,128]{2,1,0:T(1,128)S(1)} async-done(((f32[8,1,128]{2,1,0:T(1,128)}), f32[8,1,128]{2,1,0:T(1,128)S(1)}, u32[]{:S(2)}, u32[]{:S(2)}) %all-to-all-start.1) | async-done | bytes 4128 | tf_op jit(solution)/shard_map/all_to_all | solution.py:25
  93.0 0.2 fusion.67
  93.4 0.6 stack.5
  94.0 3.3 %all-to-all-start.2 = ((f32[8,2,1,8]{3,1,2,0:T(2,128)}), f32[8,2,1,8]{3,1,2,0:T(2,128)S(1)}, u32[]{:S(2)}, u32[]{:S(2)}) async-start(f32[8,2,1,8]{3,1,2,0:T(2,128)} %stack.5), calls=%async_computation.2 | async-start | bytes 16384 | tf_op jit(solution)/shard_map/all_to_all | solution.py:58
  97.5 6.3 %all-to-all-done.2 = f32[8,2,1,8]{3,1,2,0:T(2,128)S(1)} async-done(((f32[8,2,1,8]{3,1,2,0:T(2,128)}), f32[8,2,1,8]{3,1,2,0:T(2,128)S(1)}, u32[]{:S(2)}, u32[]{:S(2)}) %all-to-all-start.2) | async-done | bytes 544 | tf_op jit(solution)/shard_map/all_to_all | solution.py:58
  103.9 0.2 fusion.123
  104.2 0.2 convolution_bitcast_fusion.8
  104.4 0.2 fusion.20
  104.6 0.3 multiply_reduce_fusion.2
  105.0 0.2 convolution_bitcast_fusion.4
  105.4 0.2 convolution_bitcast_fusion.6
  105.6 17.9 %all-reduce.8 = f32[2,8,8]{2,0,1:T(2,128)S(1)} all-reduce(f32[2,8,8]{2,0,1:T(2,128)S(1)} %copy.45), channel_id=2, replica_groups=mesh['grp'=2,'row'=4,'head'=2,'br'=2] {'row','head'}, use_global_device_ids=true, to_apply=%region_14.0.clone | all-reduce | flops 128 | bytes 1024
  123.5 0.8 fusion.92
  124.4 0.4 multiply_reduce_fusion.3
  124.8 0.2 fusion.119
  125.0 2.5 %psum.38 = f32[1,8,128]{2,1,0:T(8,128)S(1)} all-reduce(f32[1,8,128]{2,1,0:T(8,128)S(1)} %add_bitcast_fusion), channel_id=1, replica_groups=mesh['grp'=2,'row'=4,'head'=2,'br'=2] {'br'}, use_global_device_ids=true, to_apply=%region_17.0 | all-reduce | flops 1024 | bytes 8192 | tf_op jit(solution)/shard_map/psum | solution.py:20
  127.5 0.6 bitcast_add_fusion.1
  128.1 3.3 %all-to-all-start.5 = ((f32[8,1,128]{2,1,0:T(1,128)}), f32[8,1,128]{2,1,0:T(1,128)S(1)}, u32[]{:S(2)}, u32[]{:S(2)}) async-start(f32[8,1,128]{2,1,0:T(1,128)} %bitcast.79), calls=%async_computation.5 | async-start | bytes 8192 | tf_op jit(solution)/shard_map/all_to_all | solution.py:25
  131.4 0.3 convolution_bitcast_fusion.15
  131.7 6.1 %all-to-all-done.5 = f32[8,1,128]{2,1,0:T(1,128)S(1)} async-done(((f32[8,1,128]{2,1,0:T(1,128)}), f32[8,1,128]{2,1,0:T(1,128)S(1)}, u32[]{:S(2)}, u32[]{:S(2)}) %all-to-all-start.5) | async-done | bytes 4128 | tf_op jit(solution)/shard_map/all_to_all | solution.py:25
  137.8 0.2 fusion.21
  138.0 0.3 multiply_reduce_fusion.1
  138.5 0.2 convolution_bitcast_fusion
  138.8 0.2 convolution_bitcast_fusion.2
  139.0 17.9 %all-reduce.9 = f32[2,8,8]{2,0,1:T(2,128)S(1)} all-reduce(f32[2,8,8]{2,0,1:T(2,128)S(1)} %copy.48), channel_id=3, replica_groups=mesh['grp'=2,'row'=4,'head'=2,'br'=2] {'row','head'}, use_global_device_ids=true, to_apply=%region_19.0.clone | all-reduce | flops 128 | bytes 1024
  157.0 0.8 fusion.91
  157.8 0.4 fusion.65
  158.2 0.2 fusion.118
  158.5 2.5 %all-reduce.10 = (f32[1,8,128]{2,1,0:T(8,128)S(1)}, f32[1,8,128]{2,1,0:T(8,128)S(1)}) all-reduce(f32[1,8,128]{2,1,0:T(8,128)S(1)} %convolution_bitcast_fusion.15, f32[1,8,128]{2,1,0:T(8,128)S(1)} %broadcast_add_fusion), channel_id=1, replica_groups=mesh['grp'=2,'row'=4,'head'=2,'br'=2] {'br'}, use_global_device_ids=true, to_apply=%region_12.0 | all-reduce | flops 2048 | bytes 16384 | tf_op jit(solution)/shard_map/psum | solution.py:20
  161.0 0.7 bitcast_add_fusion.2
  161.6 3.3 %all-to-all-start.3 = ((f32[8,1,128]{2,1,0:T(1,128)}), f32[8,1,128]{2,1,0:T(1,128)S(1)}, u32[]{:S(2)}, u32[]{:S(2)}) async-start(f32[8,1,128]{2,1,0:T(1,128)} %bitcast.56), calls=%async_computation.3 | async-start | bytes 8192 | tf_op jit(solution)/shard_map/all_to_all | solution.py:25
  164.9 0.6 bitcast_add_fusion
  165.5 5.8 %all-to-all-done.3 = f32[8,1,128]{2,1,0:T(1,128)S(1)} async-done(((f32[8,1,128]{2,1,0:T(1,128)}), f32[8,1,128]{2,1,0:T(1,128)S(1)}, u32[]{:S(2)}, u32[]{:S(2)}) %all-to-all-start.3) | async-done | bytes 4128 | tf_op jit(solution)/shard_map/all_to_all | solution.py:25
  171.3 0.6 copy.79
  (59 shorter events, 2.5 us)
Async XLA Ops:
  0.6 35.6 %copy-start = (f32[1024,128]{1,0:T(8,128)S(1)}, f32[1024,128]{1,0:T(8,128)}, u32[]{:S(2)}) copy-start(f32[1024,128]{1,0:T(8,128)} %param.18) | copy-start | bytes 1572868
  0.6 1.0 copy-start.3
  0.7 2.8 %copy-start.4 = (f32[256,64]{0,1:T(8,128)S(1)}, f32[256,64]{0,1:T(8,128)}, u32[]{:S(2)}) copy-start(f32[256,64]{0,1:T(8,128)} %param.17) | copy-start | bytes 196612
  36.9 23.6 %copy-start.8 = (s32[32,1]{0,1:T(1,128)S(1)}, s32[32,1]{0,1:T(1,128)}, u32[]{:S(2)}) copy-start(s32[32,1]{0,1:T(1,128)} %param.14) | copy-start | bytes 388
  36.9 29.5 %copy-start.1 = (f32[2,128,2,128]{3,2,1,0:T(2,128)S(1)}, f32[2,128,2,128]{3,2,1,0:T(2,128)}, u32[]{:S(2)}) copy-start(f32[2,128,2,128]{3,2,1,0:T(2,128)} %param.20) | copy-start | bytes 786436
  60.5 0.7 copy-start.6
  60.5 0.7 copy-start.7
  61.5 0.7 copy-start.5
  63.0 9.8 %all-to-all-start = ((f32[8,2,1,8]{3,1,2,0:T(2,128)}), f32[8,2,1,8]{3,1,2,0:T(2,128)S(1)}, u32[]{:S(2)}, u32[]{:S(2)}) async-start(f32[8,2,1,8]{3,1,2,0:T(2,128)} %stack.4), calls=%async_computation | async-start | bytes 16384 | tf_op jit(solution)/shard_map/all_to_all | solution.py:58
  66.4 0.7 copy-start.9
  68.5 0.7 copy-start.10
  72.8 9.7 %all-to-all-start.4 = ((f32[8,1,128]{2,1,0:T(1,128)}), f32[8,1,128]{2,1,0:T(1,128)S(1)}, u32[]{:S(2)}, u32[]{:S(2)}) async-start(f32[8,1,128]{2,1,0:T(1,128)} %bitcast.58), calls=%async_computation.4 | async-start | bytes 8192 | tf_op jit(solution)/shard_map/all_to_all | solution.py:25
  76.2 0.8 copy-start.2
  82.5 10.3 %all-to-all-start.1 = ((f32[8,1,128]{2,1,0:T(1,128)}), f32[8,1,128]{2,1,0:T(1,128)S(1)}, u32[]{:S(2)}, u32[]{:S(2)}) async-start(f32[8,1,128]{2,1,0:T(1,128)} %bitcast.34), calls=%async_computation.1 | async-start | bytes 8192 | tf_op jit(solution)/shard_map/all_to_all | solution.py:25
  94.0 9.8 %all-to-all-start.2 = ((f32[8,2,1,8]{3,1,2,0:T(2,128)}), f32[8,2,1,8]{3,1,2,0:T(2,128)S(1)}, u32[]{:S(2)}, u32[]{:S(2)}) async-start(f32[8,2,1,8]{3,1,2,0:T(2,128)} %stack.5), calls=%async_computation.2 | async-start | bytes 16384 | tf_op jit(solution)/shard_map/all_to_all | solution.py:58
  128.1 9.7 %all-to-all-start.5 = ((f32[8,1,128]{2,1,0:T(1,128)}), f32[8,1,128]{2,1,0:T(1,128)S(1)}, u32[]{:S(2)}, u32[]{:S(2)}) async-start(f32[8,1,128]{2,1,0:T(1,128)} %bitcast.79), calls=%async_computation.5 | async-start | bytes 8192 | tf_op jit(solution)/shard_map/all_to_all | solution.py:25
  161.6 9.7 %all-to-all-start.3 = ((f32[8,1,128]{2,1,0:T(1,128)}), f32[8,1,128]{2,1,0:T(1,128)S(1)}, u32[]{:S(2)}, u32[]{:S(2)}) async-start(f32[8,1,128]{2,1,0:T(1,128)} %bitcast.56), calls=%async_computation.3 | async-start | bytes 8192 | tf_op jit(solution)/shard_map/all_to_all | solution.py:25
